TPU v7x, 512 devices: a whole 4x8x8 slice. The times are simulated.
512 devices in a mesh: cx: 16 (over z_hi, y), cy: 32 (over x, z_lo, core).
Axes of the slice: x: 4, y: 8, z: 8 (z_hi: 2, z_lo: 4; z = z_hi * 4 + z_lo), core: 2. Of those that a mesh axis runs over, the one named last changes fastest.
Arguments:
- queries: bfloat16 [7, 32768, 128], P(None, ('cx', 'cy')), may hold values from -8 to 8, as said below
- keys: bfloat16 [32768, 128], P(('cx', 'cy')), may hold values from -40 to 40, as said below
- values: bfloat16 [32768, 128], P(('cx', 'cy')), may hold values from -6 to 6
Outputs:
- attended: bfloat16 [7, 32768, 128], P(None, ('cx', 'cy'))
Inputs may be any that keep to these rules, and one draw needn't show every extreme that they name: `queries`: every query is noise of about unit size in each entry plus one common direction of length 4, the same for all heads and tokens. The keys of the first four prompt positions carry a large component along the queries' common direction, so they draw much of every query's attention; all other keys are noise of about unit size in each entry.
All inputs are finite; a program needn't handle non-finite values.
Results may differ from a plain program's by a relative error of at most 0.001.
Values may be sent and summed in bfloat16 or wider, within the bound.
No kernel may reach another device: no remote copies, remote signals or barrier semaphores. Data moves between devices by JAX's collectives and lax.ppermute only.
A program may use at most 192 MiB of HBM per device.

v0:
```python
import jax
import jax.numpy as jnp
from jax import lax
from jax.sharding import Mesh
from jax.sharding import PartitionSpec as P

CX_CY = ("cx_0", "cx_1", "cy")
CX = ("cx_0", "cx_1")


masked = -1e30


def in_order(parts, dim):
    parts = jnp.moveaxis(parts, 0, dim)
    shape = parts.shape
    return parts.reshape(*shape[:dim], shape[dim] * shape[dim + 1], *shape[dim + 2 :])


def stacked_from(array, axes, sequence):
    parts = array
    for k in sequence:
        parts = lax.all_gather(parts, axes[k])
    done = sequence[::-1]
    back = [done.index(k) for k in range(len(axes))]
    parts = parts.transpose(*back, *range(len(axes), parts.ndim))
    return parts.reshape(-1, *array.shape)


def whole_of(array, axes, sequence, dim):
    return in_order(stacked_from(array, axes, sequence), dim)


def folded(array, axes, sequence, dim, update, carry):
    everything = jax.tree.map(lambda part: whole_of(part, axes, sequence, dim), array)
    return update(carry, everything, jnp.int32(0))


def attend(state, piece, start, queries_flat, query_pos, last_pos):
    keys_piece, values_piece = piece

    def update(carry):
        peak, total, mixed = carry
        head = queries_flat.shape[1]
        scores = jnp.dot(queries_flat, keys_piece.T, preferred_element_type=jnp.float32) * head ** (
            -0.5
        )
        key_pos = start + jnp.arange(keys_piece.shape[0], dtype=jnp.int32)
        visible = key_pos[None, :] <= query_pos[:, None]
        scores = jnp.where(visible, scores, masked)
        fresh = jnp.maximum(peak, jnp.max(scores, axis=1))
        shrink = jnp.exp(peak - fresh)
        weights = jnp.where(visible, jnp.exp(scores - fresh[:, None]), 0.0)
        total = total * shrink + jnp.sum(weights, axis=1)
        mixed = mixed * shrink[:, None] + jnp.dot(
            weights, values_piece.astype(jnp.float32), precision=lax.Precision.HIGHEST
        )
        return (fresh, total, mixed)

    return lax.cond(start <= last_pos, update, lambda carry: carry, state)


def per_device(queries, keys, values):
    group, tokens, head = queries.shape
    queries_flat = queries.reshape(group * tokens, head)
    here = lax.axis_index(CX_CY)
    first = here * tokens
    last_pos = first + tokens - 1
    query_pos = first + jnp.arange(group * tokens, dtype=jnp.int32) % tokens
    rows = group * tokens
    state = (
        jnp.full((rows,), masked, jnp.float32),
        jnp.zeros((rows,), jnp.float32),
        jnp.zeros((rows, head), jnp.float32),
    )

    def fold(carry, piece, start):
        return attend(carry, piece, start, queries_flat, query_pos, last_pos)

    row_keys, row_values = (
        lax.all_gather(keys, "cy", axis=0, tiled=True),
        lax.all_gather(values, "cy", axis=0, tiled=True),
    )
    state = folded((row_keys, row_values), CX, (0, 1), 0, fold, state)
    peak, total, mixed = state
    return (mixed / total[:, None]).astype(jnp.bfloat16).reshape(group, tokens, head)


def solution(mesh):
    split = Mesh(mesh.devices.reshape(2, 8, mesh.shape["cy"]), ("cx_0", "cx_1", "cy"))
    in_specs = (P(None, CX_CY, None), P(CX_CY, None), P(CX_CY, None))
    out_specs = P(None, CX_CY, None)
    return jax.shard_map(
        per_device, mesh=split, in_specs=in_specs, out_specs=out_specs, check_vma=False
    )
```

profile of v0, /device:TPU:1, one launch (start us, length us, event | category | flops | bytes accessed | tf_op | source)
XLA Modules:
  0.0 453.0 jit_solution(9957227100763392478)
XLA Ops:
  6.5 0.0 all-gather.9.cloned.1.call-start
  6.5 52.0 %all_gather.30 = bf16[2048,128]{1,0:T(8,128)(2,1)} all-gather(bf16[64,128]{1,0:T(8,128)(2,1)} %param.6), channel_id=1, replica_groups=mesh['cx_0'=2,'cx_1'=8,'cy'=32] {'cy'}, dimensions={0}, use_global_device_ids=true | all-gather | bytes 540672 | tf_op jit(solution)/shard_map/all_gather | solution.py:81
  58.6 0.0 all-gather.9.cloned.1.call-update
  58.6 0.0 all-gather.13.cloned.1.call-start
  58.6 46.8 %all_gather.35 = bf16[2048,128]{1,0:T(8,128)(2,1)} all-gather(bf16[64,128]{1,0:T(8,128)(2,1)} %param.7), channel_id=1, replica_groups=mesh['cx_0'=2,'cx_1'=8,'cy'=32] {'cy'}, dimensions={0}, use_global_device_ids=true | all-gather | bytes 540672 | tf_op jit(solution)/shard_map/all_gather | solution.py:82
  105.4 0.0 all-gather.13.cloned.1.call-update
  105.5 0.0 all-gather.11.cloned.1.call-start
  105.5 0.8 all-gather.9.cloned.1.call-done
  106.3 0.0 all-gather.11.cloned.1.call-update
  106.3 0.0 all-gather.15.cloned.1.call-start
  106.4 47.6 %all-gather.13.cloned.1.call-done = bf16[4096,128]{1,0:T(8,128)(2,1)} async-done(((bf16[2048,128]{1,0:T(8,128)(2,1)}), bf16[4096,128]{1,0:T(8,128)(2,1)}) %all-gather.13.cloned.1.call-update) | async-done | bytes 1048592 | tf_op jit(solution)/shard_map/all_gather | solution.py:23
  154.0 0.0 all-gather.15.cloned.1.call-update
  154.1 94.9 %all-gather.11.cloned.1.call-done = bf16[16,2048,128]{2,1,0:T(8,128)(2,1)} async-done(((bf16[2,2048,128]{2,1,0:T(8,128)(2,1)}), bf16[16,2048,128]{2,1,0:T(8,128)(2,1)}) %all-gather.11.cloned.1.call-update) | async-done | bytes 8388624 | tf_op jit(solution)/shard_map/all_gather | solution.py:23
  248.9 97.3 %all-gather.15.cloned.1.call-done = bf16[16,2048,128]{2,1,0:T(8,128)(2,1)} async-done(((bf16[2,2048,128]{2,1,0:T(8,128)(2,1)}), bf16[16,2048,128]{2,1,0:T(8,128)(2,1)}) %all-gather.15.cloned.1.call-update) | async-done | bytes 8388624 | tf_op jit(solution)/shard_map/all_gather | solution.py:23
  346.2 99.5 %conditional.1 = (f32[448]{0:T(512)S(1)}, f32[448,128]{1,0:T(8,128)S(1)}) conditional(s32[]{:T(128)} %convert_element_type.7, () %tuple.20, (s32[]{:T(128)}, s32[448]{0:T(512)S(1)}, bf16[7,64,128]{2,1,0:T(8,128)(2,1)}, bf16[2,8,2048,128]{3,2,0,1:T(8,128)(2,1)}, bf16[2,8,2048,128]{3,2,0,1:T(8,128)(2,1)}) %tuple.37), branch_computations={%region_0.1_spmd, %region_1.4_spmd} | conditional | flops 26468216832 | bytes 226865168 | solution.py:60
  346.2 7.5 %copy.7 = bf16[2,8,2048,128]{3,2,1,0:T(8,128)(2,1)} copy(bf16[2,8,2048,128]{3,2,0,1:T(8,128)(2,1)} %get-tuple-element.91) | data formatting | bytes 16777216 | tf_op jit(solution)/shard_map
  353.7 24.8 %fusion.9 = (f32[448]{0:T(512)S(1)}, f32[448,32768]{1,0:T(8,128)}) fusion(bf16[448,128]{1,0:T(8,128)(2,1)} %bitcast.21, bf16[32768,128]{1,0:T(8,128)(2,1)} %bitcast.18, s32[448]{0:T(512)S(1)} %fusion.6), kind=kOutput, calls=%fused_computation.16 | convolution fusion | flops 3816816128 | bytes 67227136 | tf_op jit(solution)/shard_map/cond/branch_1_fun/dot_general | solution.py:45
  378.6 19.0 %fusion.1 = f32[448]{0:T(512)S(1)} fusion(f32[448,32768]{1,0:T(8,128)} %get-tuple-element.96, f32[448]{0:T(512)S(1)} %broadcast_maximum_fusion, s32[448]{0:T(512)S(1)} %fusion.6), kind=kLoop, calls=%fused_computation.4 | loop fusion | flops 58719808 | bytes 58725632 | tf_op jit(solution)/shard_map/cond/branch_1_fun/reduce_sum | solution.py:54
  397.6 7.5 %copy.8 = bf16[2,8,2048,128]{3,2,1,0:T(8,128)(2,1)} copy(bf16[2,8,2048,128]{3,2,0,1:T(8,128)(2,1)} %get-tuple-element.92) | data formatting | bytes 16777216 | tf_op jit(solution)/shard_map
  405.1 40.6 %fusion.5 = f32[448,128]{1,0:T(8,128)S(1)} fusion(bf16[32768,128]{1,0:T(8,128)(2,1)} %bitcast.17, f32[448,32768]{1,0:T(8,128)} %get-tuple-element.96, f32[448]{0:T(512)S(1)} %broadcast_maximum_fusion, s32[448]{0:T(512)S(1)} %fusion.6, f32[448]{0:T(512)S(1)} %get-tuple-element.93), kind=kOutput, calls=%fused_computation.8 | convolution fusion | flops 22592675840 | bytes 67343616 | tf_op jit(solution)/shard_map/cond/branch_1_fun/dot_general | solution.py:55
  445.7 0.8 divide_convert_fusion
  (4 shorter events, 0.0 us)
Async XLA Ops:
  6.5 99.8 %all-gather.9.cloned.1.call-start = ((), (), s32[]{:S(2)}) async-start(), calls=%async_computation | async-start | bytes 1572864 | tf_op jit(solution)/shard_map/all_gather | solution.py:23
  58.6 95.4 %all-gather.13.cloned.1.call-start = ((), (), s32[]{:S(2)}) async-start(), calls=%async_computation.2 | async-start | bytes 1572864 | tf_op jit(solution)/shard_map/all_gather | solution.py:23
  105.5 143.5 %all-gather.11.cloned.1.call-start = ((), (), s32[]{:S(2)}) async-start(), calls=%async_computation.1 | async-start | bytes 9437184 | tf_op jit(solution)/shard_map/all_gather | solution.py:23
  106.3 239.9 %all-gather.15.cloned.1.call-start = ((), (), s32[]{:S(2)}) async-start(), calls=%async_computation.3 | async-start | bytes 9437184 | tf_op jit(solution)/shard_map/all_gather | solution.py:23
Sparse Core Ops, SparseCore 0:
  58.7 47.5 all-gather.8
  108.4 45.5 all-gather.12
  156.1 92.7 all-gather.10
  250.9 95.3 all-gather.14
where the time goes:
time: 453 us
  waiting for transfers between devices  241 us (53%)
  blocking collectives  98.8 us (22%)
  matrix products  65.5 us (14%)
  other arithmetic  19.8 us (4%)
  local copies, waits for them, and re-layouts  15 us (3%)
  between operations  13.1 us (3%)
    all_gather x4, waiting for transfers between devices, stacked_from(): parts = lax.all_gather(parts, axes[k])  241 us
    all_gather x1, blocking collectives, per_device(): lax.all_gather(keys, 'cy', axis=0, tiled=True)  52 us
    all_gather x1, blocking collectives, per_device(): lax.all_gather(values, 'cy', axis=0, tiled=True)  46.8 us
    dot_general x1, matrix products, update(): jnp.dot(weights, values_piece.astype(jnp.float32), precision=lax.Precisio...  40.6 us
    dot_general x1, matrix products, update(): jnp.dot(queries_flat, keys_piece.T, preferred_element_type=jnp.float32)  24.8 us
    reduce_sum x1, other arithmetic, update(): total = total * shrink + jnp.sum(weights, axis=1)  19 us
    another operation x2, local copies, waits for them, and re-layouts  15 us
  transfers between devices with their start and end apart: 4, of which 4 were waited for; matrix products, arithmetic and copies ran while one was open for 0% of the time, Pallas kernels for 0%

commit v1 on v0

v1 whole, which is shorter than its diff:
```python
import math

import jax
import jax.numpy as jnp
from jax import lax
from jax.experimental import pallas as pl
from jax.experimental.pallas import tpu as pltpu
from jax.sharding import Mesh
from jax.sharding import PartitionSpec as P

AXES = ("zh", "y", "x", "zl", "c")
SIZES = (2, 8, 4, 4, 2)
TEAM = ("x", "c")
Z = ("zh", "zl")

HEAD = 128
GROUP = 7
TOK = 64
ROWS = GROUP * TOK
MATES = 8
SINKS = 4
ALL_ROWS = MATES * ROWS
LANES = 256
STAT = ROWS
EXTRA = STAT + 16 * GROUP
PAYLOAD = EXTRA + 16
masked = -(2.0**100)
SCALE = HEAD**-0.5 * math.log2(math.e)
f32 = jnp.float32
bf16 = jnp.bfloat16


def place():
    return tuple(lax.axis_index(name) for name in AXES)


def attend_kernel(at, q_ref, kv_ref, out_ref, vt_ref):
    zh, y, x, zl, c = (at[i] for i in range(5))
    span = zh * 8 + y
    ones = jnp.ones((16, 256), bf16)

    def turn(tile, carry):
        v = kv_ref[tile // 8, :, tile % 8, :, HEAD:].reshape(256, HEAD)
        vt_ref[tile] = jnp.concatenate([v.astype(f32).T.astype(bf16), ones], axis=0)
        return carry

    lax.fori_loop(0, span + 1, turn, 0)

    def rows_tile(i, carry):
        q = q_ref[pl.ds(pl.multiple_of(i * LANES, LANES), LANES), :]

        def scores_of(tile):
            k = kv_ref[tile // 8, :, tile % 8, :, :HEAD].reshape(256, HEAD)
            return lax.dot_general(k, q, (((1,), (1,)), ((), ())), preferred_element_type=f32) * SCALE

        def fold(tile, state, scores, visible):
            peak, mixed = state
            if visible is not None:
                scores = jnp.where(visible, scores, masked)
            fresh = jnp.maximum(peak, jnp.max(scores, axis=0, keepdims=True))
            weights = jnp.exp2(scores - fresh)
            if visible is not None:
                weights = jnp.where(visible, weights, 0.0)
            update = jnp.dot(vt_ref[tile], weights.astype(bf16), preferred_element_type=f32)
            return fresh, mixed * jnp.exp2(peak - fresh) + update

        def plain(tile, state):
            return fold(tile, state, scores_of(tile), None)

        def edge(tile, state):
            row = i * LANES + lax.broadcasted_iota(jnp.int32, (1, LANES), 1)
            mate = sum((row >= ROWS * n).astype(jnp.int32) for n in range(1, MATES))
            block = span * 32 + (mate >> 1) * 8 + zl * 2 + (mate & 1)
            query_pos = block * TOK + (row & (TOK - 1))
            key = lax.broadcasted_iota(jnp.int32, (256, 1), 0)
            key_pos = (tile * 32 + x * 8 + (key >> 6) * 2 + c) * TOK + (key & (TOK - 1))
            visible = (key_pos <= query_pos) & (key_pos >= SINKS)
            return fold(tile, state, scores_of(tile), visible)

        state = (jnp.full((1, LANES), masked, f32), jnp.zeros((HEAD + 16, LANES), f32))
        state = edge(0, state)
        state = lax.fori_loop(1, span, plain, state)
        state = lax.fori_loop(jnp.maximum(span, 1), span + 1, edge, state)
        peak, mixed = state
        sent = peak.astype(bf16)
        mixed = mixed * jnp.exp2(peak - sent.astype(f32))
        total = mixed[HEAD : HEAD + 1]
        high = total.astype(bf16)
        low = (total - high.astype(f32)).astype(bf16)
        stat = jnp.concatenate([sent, high, low, jnp.zeros((13, LANES), bf16)], axis=0)
        turned = mixed[:HEAD].T.astype(bf16)
        for part in range(LANES // TOK):
            piece = i * (LANES // TOK) + part
            mate = piece // GROUP
            head = piece - mate * GROUP
            out_ref[mate, pl.ds(pl.multiple_of(head * TOK, TOK), TOK), :] = turned[part * TOK : (part + 1) * TOK]
            lanes = slice(part // 2 * 128, part // 2 * 128 + 128)
            out_ref[mate, pl.ds(pl.multiple_of(STAT + head * 16, 16), 16), :] = stat[:, lanes]
        return carry

    lax.fori_loop(0, ALL_ROWS // LANES, rows_tile, 0)
    first = kv_ref[0, 0, 0, :8, :].astype(f32)
    both = jnp.concatenate([first[:SINKS, :HEAD], first[:SINKS, HEAD:], jnp.zeros((8, HEAD), f32)], axis=0).astype(bf16)
    for mate in range(MATES):
        out_ref[mate, EXTRA:, :] = both


def combine_kernel(at, q_ref, got_ref, out_ref, turn_ref):
    zh, y, x, zl, c = (at[i] for i in range(5))
    mate = x * 2 + c
    first = ((zh * 8 + y) * 32 + x * 8 + zl * 2 + c) * TOK
    extra = got_ref[0, EXTRA:, :]
    values = extra.astype(f32)
    for head in range(GROUP):
        q = q_ref[head * TOK : (head + 1) * TOK, :]
        twice = jnp.concatenate([q, q], axis=0)
        scores = lax.dot_general(extra, twice, (((1,), (1,)), ((), ())), preferred_element_type=f32)[:8] * SCALE
        number = lax.broadcasted_iota(jnp.int32, (8, 128), 0)
        token = lax.broadcasted_iota(jnp.int32, (8, 128), 1) & (TOK - 1)
        visible = (number < SINKS) & (number <= first + token)
        scores = jnp.where(visible, scores, masked)
        stats = [got_ref[k, STAT + head * 16 : STAT + head * 16 + 16, :].astype(f32) for k in range(MATES)]
        peaks = jnp.concatenate([s[0:1] for s in stats], axis=0)
        totals = jnp.concatenate([s[1:2] + s[2:3] for s in stats], axis=0)
        peak = jnp.maximum(jnp.max(scores, axis=0, keepdims=True), jnp.max(peaks, axis=0, keepdims=True))
        sinks = jnp.where(visible, jnp.exp2(scores - peak), 0.0)
        shares = jnp.exp2(peaks - peak)
        total = jnp.sum(sinks, axis=0, keepdims=True) + jnp.sum(shares * totals, axis=0, keepdims=True)
        table = jnp.concatenate([shares / total, sinks / total, jnp.zeros((112, 128), f32)], axis=0)
        turn_ref[...] = table.T
        half = pl.multiple_of(((mate + head) & 1) * TOK, TOK)
        factors = turn_ref[pl.ds(half, TOK), :]
        mixed = jnp.zeros((TOK, HEAD), f32)
        for k in range(MATES):
            mixed = mixed + factors[:, k : k + 1] * got_ref[k, head * TOK : (head + 1) * TOK, :].astype(f32)
        for s in range(SINKS):
            mixed = mixed + factors[:, MATES + s : MATES + s + 1] * values[SINKS + s : SINKS + s + 1, :]
        out_ref[head * TOK : (head + 1) * TOK, :] = mixed.astype(bf16)


def everyone(block, axes, count):
    copies = jnp.broadcast_to(block[None], (count, *block.shape))
    return lax.all_to_all(copies, axes, 0, 0, tiled=True)


def per_device(queries, keys, values):
    at = jnp.stack(place()).astype(jnp.int32)
    q = queries.reshape(ROWS, HEAD)
    q_all = lax.all_gather(q, TEAM, axis=0, tiled=True)
    kv = jnp.concatenate([keys, values], axis=1)
    kv = everyone(kv, "y", 8)
    kv = everyone(kv, Z, 8).reshape(2, 4, 8, TOK, 2 * HEAD)
    smem = pl.BlockSpec(memory_space=pltpu.SMEM)
    vmem = pl.BlockSpec(memory_space=pltpu.VMEM)
    partial = pl.pallas_call(
        attend_kernel,
        out_shape=jax.ShapeDtypeStruct((MATES, PAYLOAD, HEAD), bf16),
        in_specs=[smem, vmem, vmem],
        out_specs=vmem,
        scratch_shapes=[pltpu.VMEM((16, HEAD + 16, 256), bf16)],
        name="attend",
    )(at, q_all, kv)
    got = lax.all_to_all(partial, TEAM, 0, 0, tiled=True)
    out = pl.pallas_call(
        combine_kernel,
        out_shape=jax.ShapeDtypeStruct((ROWS, HEAD), bf16),
        in_specs=[smem, vmem, vmem],
        out_specs=vmem,
        scratch_shapes=[pltpu.VMEM((128, 128), f32)],
        name="combine",
    )(at, q, got)
    return out.reshape(GROUP, TOK, HEAD)


def solution(mesh):
    split = Mesh(mesh.devices.reshape(SIZES), AXES)
    shard = P(None, AXES, None)
    return jax.shard_map(
        per_device,
        mesh=split,
        in_specs=(shard, P(AXES, None), P(AXES, None)),
        out_specs=shard,
        check_vma=False,
    )
```

time: 453 us -> 202 us (0.45)
  the two profiles are of different devices: /device:TPU:1 before, /device:TPU:440 now
where the time goes in v1:
time: 202 us
  Pallas kernels  110 us (54%)
  blocking collectives  51.4 us (25%)
  waiting for transfers between devices  30.6 us (15%)
  starting transfers between devices  5.55 us (3%)
  local copies, waits for them, and re-layouts  3.53 us (2%)
    pallas_call x1, Pallas kernels, per_device(): pl.pallas_call(attend_kernel, out_shape=jax.ShapeDtypeStruct((MATES, PAYL...  106 us
    all_to_all x1, waiting for transfers between devices, everyone(): return lax.all_to_all(copies, axes, 0, 0, tiled=True)  30.6 us
    all_to_all x1, blocking collectives, per_device(): got = lax.all_to_all(partial, TEAM, 0, 0, tiled=True)  21.8 us
    all_gather x1, blocking collectives, per_device(): q_all = lax.all_gather(q, TEAM, axis=0, tiled=True)  14.9 us
    all_to_all x1, blocking collectives, everyone(): return lax.all_to_all(copies, axes, 0, 0, tiled=True)  14.7 us
    all_to_all x1, starting transfers between devices, everyone(): return lax.all_to_all(copies, axes, 0, 0, tiled=True)  5.55 us
  transfers between devices with their start and end apart: 1, of which 1 were waited for; matrix products, arithmetic and copies ran while one was open for 0% of the time, Pallas kernels for 0%

profile of v1, /device:TPU:440, one launch (start us, length us, event | category | flops | bytes accessed | tf_op | source)
XLA Modules:
  0.0 201.6 jit_solution(12240367723141627930)
XLA Ops:
  0.0 0.7 pad_maximum_fusion
  0.8 14.7 %all_to_all.15 = bf16[8,64,256]{2,1,0:T(8,128)(2,1)S(1)} all-to-all(bf16[8,64,256]{2,1,0:T(8,128)(2,1)S(1)} %broadcast_in_dim.4), channel_id=1, replica_groups=mesh['zh'=2,'y'=8,'x'=4,'zl'=4,'c'=2] {'y'}, dimensions={0} | all-to-all | bytes 524288 | tf_op jit(solution)/shard_map/all_to_all | solution.py:143
  15.5 1.6 broadcast_in_dim.5
  17.1 0.0 copy-start.1
  17.1 5.6 %all-to-all-start.1 = ((bf16[8,8,64,256]{3,2,1,0:T(8,128)(2,1)}), bf16[8,8,64,256]{3,2,1,0:T(8,128)(2,1)S(1)}, u32[]{:S(2)}, u32[]{:S(2)}) async-start(bf16[8,8,64,256]{3,2,1,0:T(8,128)(2,1)} %broadcast_in_dim.5), calls=%async_computation.1 | async-start | bytes 4194304 | tf_op jit(solution)/shard_map/all_to_all | solution.py:143
  22.6 0.6 stack.23.at
  23.2 0.0 copy-done.1
  23.2 14.9 %all_gather.3.q_ref = bf16[3584,128]{1,0:T(8,128)(2,1)} all-gather(bf16[448,128]{1,0:T(8,128)(2,1)S(1)} %bitcast.10), channel_id=1, replica_groups=mesh['zh'=2,'y'=8,'x'=4,'zl'=4,'c'=2] {'x','c'}, dimensions={0}, use_global_device_ids=true | all-gather | bytes 1032192 | tf_op jit(solution)/shard_map/all_gather | solution.py:149
  38.2 30.6 %all-to-all-done.1 = bf16[8,8,64,256]{3,2,1,0:T(8,128)(2,1)S(1)} async-done(((bf16[8,8,64,256]{3,2,1,0:T(8,128)(2,1)}), bf16[8,8,64,256]{3,2,1,0:T(8,128)(2,1)S(1)}, u32[]{:S(2)}, u32[]{:S(2)}) %all-to-all-start.1) | async-done | bytes 2097184 | tf_op jit(solution)/shard_map/all_to_all | solution.py:143
  68.8 0.0 copy-start
  68.8 1.3 copy-done
  70.1 106.3 %attend.1 = bf16[8,576,128]{2,1,0:T(8,128)(2,1)} custom-call(s32[5]{0:T(128)} %stack.23.at, bf16[3584,128]{1,0:T(8,128)(2,1)} %all_gather.3.q_ref, bf16[2,4,8,64,256]{4,3,2,1,0:T(8,128)(2,1)} %bitcast.8), custom_call_target="tpu_custom_call" | custom-call | tf_op jit(solution)/shard_map/attend/pallas_call | solution.py:155
  176.4 21.8 %all_to_all.16.got_ref = bf16[8,576,128]{2,1,0:T(8,128)(2,1)} all-to-all(bf16[8,576,128]{2,1,0:T(8,128)(2,1)} %attend.1), channel_id=1, replica_groups=mesh['zh'=2,'y'=8,'x'=4,'zl'=4,'c'=2] {'x','c'}, dimensions={0} | all-to-all | bytes 2359296 | tf_op jit(solution)/shard_map/all_to_all | solution.py:163
  198.1 3.5 %combine.1 = bf16[448,128]{1,0:T(8,128)(2,1)} custom-call(s32[5]{0:T(128)} %stack.23.at, bf16[448,128]{1,0:T(8,128)(2,1)} %bitcast.9, bf16[8,576,128]{2,1,0:T(8,128)(2,1)} %all_to_all.16.got_ref), custom_call_target="tpu_custom_call" | custom-call | tf_op jit(solution)/shard_map/combine/pallas_call | solution.py:164
  (1 shorter events, 0.0 us)
Async XLA Ops:
  17.1 6.1 %copy-start.1 = (bf16[7,64,128]{2,1,0:T(8,128)(2,1)S(1)}, bf16[7,64,128]{2,1,0:T(8,128)(2,1)}, u32[]{:S(2)}) copy-start(bf16[7,64,128]{2,1,0:T(8,128)(2,1)} %param.3) | copy-start | bytes 344068
  17.1 51.7 %all-to-all-start.1 = ((bf16[8,8,64,256]{3,2,1,0:T(8,128)(2,1)}), bf16[8,8,64,256]{3,2,1,0:T(8,128)(2,1)S(1)}, u32[]{:S(2)}, u32[]{:S(2)}) async-start(bf16[8,8,64,256]{3,2,1,0:T(8,128)(2,1)} %broadcast_in_dim.5), calls=%async_computation.1 | async-start | bytes 4194304 | tf_op jit(solution)/shard_map/all_to_all | solution.py:143
  68.8 1.3 copy-start

commit v2 on v1

v2 whole, which is shorter than its diff:
```python
import math

import jax
import jax.numpy as jnp
from jax import lax
from jax.experimental import pallas as pl
from jax.experimental.pallas import tpu as pltpu
from jax.sharding import Mesh
from jax.sharding import PartitionSpec as P

AXES = ("zh", "y", "x", "zl", "c")
SIZES = (2, 8, 4, 4, 2)
TEAM = ("x", "c")
Z = ("zh", "zl")

HEAD = 128
GROUP = 7
TOK = 64
ROWS = GROUP * TOK
MATES = 8
SINKS = 4
ALL_ROWS = MATES * ROWS
STAT = ROWS
CHUNKS = 4
EXTRA = STAT + 16 * CHUNKS
PAYLOAD = EXTRA + 16
masked = -(2.0**100)
SCALE = HEAD**-0.5 * math.log2(math.e)
f32 = jnp.float32
bf16 = jnp.bfloat16


def place():
    return tuple(lax.axis_index(name) for name in AXES)


def attend_kernel(at, q_ref, kv_ref, out_ref, sum_ref, peak_ref):
    zh, y, x, zl, c = (at[i] for i in range(5))
    span = zh * 8 + y

    def keys_of(tile):
        return kv_ref[tile // 8, :, tile % 8, :, :HEAD].reshape(256, HEAD)

    def values_of(tile):
        v = kv_ref[tile // 8, :, tile % 8, :, HEAD:].reshape(256, HEAD)
        return jnp.concatenate([v, jnp.ones((256, HEAD), bf16)], axis=1)

    def rows_of(mate):
        if isinstance(mate, int):
            return slice(mate * ROWS, (mate + 1) * ROWS)
        return pl.ds(pl.multiple_of(mate * ROWS, ROWS), ROWS)

    def scores_of(k, mate):
        q = q_ref[rows_of(mate), :]
        return lax.dot_general(q, k, (((1,), (1,)), ((), ())), preferred_element_type=f32) * SCALE

    def visible_of(tile, mate):
        block = span * 32 + (mate >> 1) * 8 + zl * 2 + (mate & 1)
        query_pos = block * TOK + lax.broadcasted_iota(jnp.int32, (TOK, 1), 0)
        key = lax.broadcasted_iota(jnp.int32, (1, 256), 1)
        key_pos = (tile * 32 + x * 8 + (key >> 6) * 2 + c) * TOK + (key & (TOK - 1))
        return (key_pos <= query_pos) & (key_pos >= SINKS)

    def keep(visible, array, other):
        array = array.reshape(GROUP, TOK, 256)
        return jnp.where(visible[None], array, other).reshape(ROWS, 256)

    def shifted(scores, mate):
        peak = peak_ref[rows_of(mate), :]
        return jnp.exp2(scores - jnp.concatenate([peak] * (scores.shape[1] // HEAD), axis=1))

    def mix(weights, v):
        return jnp.dot(weights.astype(bf16), v, preferred_element_type=f32)

    k, v = keys_of(0), values_of(0)
    for mate in range(MATES):
        visible = visible_of(0, mate)
        scores = keep(visible, scores_of(k, mate), masked)
        peak = jnp.max(scores, axis=1, keepdims=True).astype(bf16).astype(f32)
        peak_ref[rows_of(mate), :] = jnp.broadcast_to(peak, (ROWS, HEAD))
        sum_ref[rows_of(mate), :] = mix(keep(visible, shifted(scores, mate), 0.0), v)

    pairs = jnp.maximum(span - 1, 0) // 2

    def pair(number, carry):
        tile = 1 + 2 * number
        k = jnp.concatenate([keys_of(tile), keys_of(tile + 1)], axis=0)
        v = jnp.concatenate([values_of(tile), values_of(tile + 1)], axis=0)
        for mate in range(MATES):
            sum_ref[rows_of(mate), :] += mix(shifted(scores_of(k, mate), mate), v)
        return carry

    lax.fori_loop(0, pairs, pair, 0)

    def edge(tile, carry):
        k, v = keys_of(tile), values_of(tile)
        for mate in range(MATES):
            weights = shifted(scores_of(k, mate), mate)
            sum_ref[rows_of(mate), :] += mix(keep(visible_of(tile, mate), weights, 0.0), v)
        return carry

    lax.fori_loop(1 + 2 * pairs, span + 1, edge, 0)

    @pl.when(jnp.logical_not(jnp.max(sum_ref[:, HEAD:]) < 2.0**120))
    def _():
        def mate_rows(mate, carry):
            rows = rows_of(mate)
            peak_ref[rows, :] = jnp.full((ROWS, HEAD), masked, f32)
            sum_ref[rows, :] = jnp.zeros((ROWS, 2 * HEAD), f32)

            def step(tile, carry):
                visible = visible_of(tile, mate)
                scores = keep(visible, scores_of(keys_of(tile), mate), masked)
                top = jnp.max(scores, axis=1, keepdims=True)
                old = peak_ref[rows, :]
                peak = jnp.maximum(old, jnp.broadcast_to(top, (ROWS, HEAD)))
                peak_ref[rows, :] = peak
                shrink = jnp.exp2(old - peak)
                fresh = mix(keep(visible, shifted(scores, mate), 0.0), values_of(tile))
                sum_ref[rows, :] = sum_ref[rows, :] * jnp.concatenate([shrink, shrink], axis=1) + fresh
                return carry

            lax.fori_loop(0, span + 1, step, 0)
            peak = peak_ref[rows, :]
            sent = peak.astype(bf16).astype(f32)
            shrink = jnp.exp2(peak - sent)
            peak_ref[rows, :] = sent
            sum_ref[rows, :] = sum_ref[rows, :] * jnp.concatenate([shrink, shrink], axis=1)
            return carry

        lax.fori_loop(0, MATES, mate_rows, 0)

    lane = lax.broadcasted_iota(jnp.int32, (1, HEAD), 1)
    first = kv_ref[0, 0, 0, :8, :].astype(f32)
    both = jnp.concatenate([first[:SINKS, :HEAD], first[:SINKS, HEAD:], jnp.zeros((8, HEAD), f32)], axis=0).astype(bf16)
    for mate in range(MATES):
        out_ref[mate, :ROWS, :] = sum_ref[rows_of(mate), :HEAD].astype(bf16)
        total = sum_ref[rows_of(mate), HEAD:]
        high = total.astype(bf16).astype(f32)
        stat = jnp.where(lane == 0, peak_ref[rows_of(mate), :], jnp.where(lane == 1, high, total - high))
        stat = jnp.concatenate([stat, jnp.zeros((TOK, HEAD), f32)], axis=0)
        for chunk in range(CHUNKS):
            turned = stat[chunk * 128 : (chunk + 1) * 128].T
            out_ref[mate, STAT + 16 * chunk : STAT + 16 * (chunk + 1), :] = turned[:16].astype(bf16)
        out_ref[mate, EXTRA:, :] = both


def combine_kernel(at, q_ref, got_ref, out_ref):
    zh, y, x, zl, c = (at[i] for i in range(5))
    first = ((zh * 8 + y) * 32 + x * 8 + zl * 2 + c) * TOK
    extra = got_ref[0, EXTRA:, :]
    values = extra.astype(f32)
    number = lax.broadcasted_iota(jnp.int32, (8, 128), 0)
    token = lax.broadcasted_iota(jnp.int32, (8, 128), 1) & (TOK - 1)
    visible = (number < SINKS) & (number <= first + token)
    for chunk in range(CHUNKS):
        size = min(128, ROWS - 128 * chunk)
        rows = slice(128 * chunk, 128 * chunk + size)
        q = q_ref[rows, :]
        if size < 128:
            q = jnp.concatenate([q, q], axis=0)
        scores = lax.dot_general(extra, q, (((1,), (1,)), ((), ())), preferred_element_type=f32)[:8] * SCALE
        scores = jnp.where(visible, scores, masked)
        at_row = STAT + 16 * chunk
        stats = [got_ref[k, at_row : at_row + 16, :].astype(f32) for k in range(MATES)]
        peaks = jnp.concatenate([s[0:1] for s in stats], axis=0)
        totals = jnp.concatenate([s[1:2] + s[2:3] for s in stats], axis=0)
        peak = jnp.maximum(jnp.max(scores, axis=0, keepdims=True), jnp.max(peaks, axis=0, keepdims=True))
        sinks = jnp.where(visible, jnp.exp2(scores - peak), 0.0)
        shares = jnp.exp2(peaks - peak)
        total = jnp.sum(sinks, axis=0, keepdims=True) + jnp.sum(shares * totals, axis=0, keepdims=True)
        table = jnp.concatenate([shares / total, sinks / total, jnp.zeros((112, 128), f32)], axis=0)
        factors = table.T[:size]
        mixed = jnp.zeros((size, HEAD), f32)
        for k in range(MATES):
            mixed = mixed + factors[:, k : k + 1] * got_ref[k, rows, :].astype(f32)
        for s in range(SINKS):
            mixed = mixed + factors[:, MATES + s : MATES + s + 1] * values[SINKS + s : SINKS + s + 1, :]
        out_ref[rows, :] = mixed.astype(bf16)


def everyone(block, axes, count):
    copies = jnp.broadcast_to(block[None], (count, *block.shape))
    return lax.all_to_all(copies, axes, 0, 0, tiled=True)


def per_device(queries, keys, values):
    at = jnp.stack(place()).astype(jnp.int32)
    q = queries.reshape(ROWS, HEAD)
    q_all = lax.all_gather(q, TEAM, axis=0, tiled=True)
    kv = jnp.concatenate([keys, values], axis=1)
    kv = everyone(kv, "y", 8)
    kv = everyone(kv, Z, 8).reshape(2, 4, 8, TOK, 2 * HEAD)
    smem = pl.BlockSpec(memory_space=pltpu.SMEM)
    vmem = pl.BlockSpec(memory_space=pltpu.VMEM)
    partial = pl.pallas_call(
        attend_kernel,
        out_shape=jax.ShapeDtypeStruct((MATES, PAYLOAD, HEAD), bf16),
        in_specs=[smem, vmem, vmem],
        out_specs=vmem,
        scratch_shapes=[pltpu.VMEM((ALL_ROWS, 2 * HEAD), f32), pltpu.VMEM((ALL_ROWS, HEAD), f32)],
        name="attend",
    )(at, q_all, kv)
    got = lax.all_to_all(partial, TEAM, 0, 0, tiled=True)
    out = pl.pallas_call(
        combine_kernel,
        out_shape=jax.ShapeDtypeStruct((ROWS, HEAD), bf16),
        in_specs=[smem, vmem, vmem],
        out_specs=vmem,
        name="combine",
    )(at, q, got)
    return out.reshape(GROUP, TOK, HEAD)


def solution(mesh):
    split = Mesh(mesh.devices.reshape(SIZES), AXES)
    shard = P(None, AXES, None)
    return jax.shard_map(
        per_device,
        mesh=split,
        in_specs=(shard, P(AXES, None), P(AXES, None)),
        out_specs=shard,
        check_vma=False,
    )
```

time: 202 us -> 118 us (0.58)
  the two profiles are of different devices: /device:TPU:440 before, /device:TPU:369 now
where the time goes in v2:
time: 118 us
  blocking collectives  54.7 us (46%)
  waiting for transfers between devices  28.7 us (24%)
  Pallas kernels  24.1 us (20%)
  starting transfers between devices  5.9 us (5%)
  local copies, waits for them, and re-layouts  3.57 us (3%)
    all_to_all x1, waiting for transfers between devices, everyone(): return lax.all_to_all(copies, axes, 0, 0, tiled=True)  28.7 us
    all_to_all x1, blocking collectives, per_device(): got = lax.all_to_all(partial, TEAM, 0, 0, tiled=True)  23.9 us
    pallas_call x1, Pallas kernels, per_device(): pl.pallas_call(attend_kernel, out_shape=jax.ShapeDtypeStruct((MATES, PAYL...  20.9 us
    all_gather x1, blocking collectives, per_device(): q_all = lax.all_gather(q, TEAM, axis=0, tiled=True)  16 us
    all_to_all x1, blocking collectives, everyone(): return lax.all_to_all(copies, axes, 0, 0, tiled=True)  14.8 us
    all_to_all x1, starting transfers between devices, everyone(): return lax.all_to_all(copies, axes, 0, 0, tiled=True)  5.9 us
    pallas_call x1, Pallas kernels, per_device(): pl.pallas_call(combine_kernel, out_shape=jax.ShapeDtypeStruct((ROWS, HEAD...  3.18 us
  transfers between devices with their start and end apart: 1, of which 1 were waited for; matrix products, arithmetic and copies ran while one was open for 1% of the time, Pallas kernels for 0%

profile of v2, /device:TPU:369, one launch (start us, length us, event | category | flops | bytes accessed | tf_op | source)
XLA Modules:
  0.0 117.7 jit_solution(7625941766565200598)
XLA Ops:
  0.0 0.7 pad_maximum_fusion
  0.8 14.8 %all_to_all.15 = bf16[8,64,256]{2,1,0:T(8,128)(2,1)S(1)} all-to-all(bf16[8,64,256]{2,1,0:T(8,128)(2,1)S(1)} %broadcast_in_dim.4), channel_id=1, replica_groups=mesh['zh'=2,'y'=8,'x'=4,'zl'=4,'c'=2] {'y'}, dimensions={0} | all-to-all | bytes 524288 | tf_op jit(solution)/shard_map/all_to_all | solution.py:184
  15.5 1.6 %broadcast_in_dim.5 = bf16[8,8,64,256]{3,2,1,0:T(8,128)(2,1)} broadcast(bf16[8,64,256]{2,1,0:T(8,128)(2,1)S(1)} %all_to_all.15), dimensions={1,2,3} | broadcast | bytes 2359296 | tf_op jit(solution)/shard_map/broadcast_in_dim | solution.py:183
  17.1 0.0 copy-start.1
  17.1 5.9 %all-to-all-start.1 = ((bf16[8,8,64,256]{3,2,1,0:T(8,128)(2,1)}), bf16[8,8,64,256]{3,2,1,0:T(8,128)(2,1)S(1)}, u32[]{:S(2)}, u32[]{:S(2)}) async-start(bf16[8,8,64,256]{3,2,1,0:T(8,128)(2,1)} %broadcast_in_dim.5), calls=%async_computation.1 | async-start | bytes 4194304 | tf_op jit(solution)/shard_map/all_to_all | solution.py:184
  23.0 0.6 stack.23.at
  23.7 0.0 copy-done.1
  23.7 16.0 %all_gather.3.q_ref = bf16[3584,128]{1,0:T(8,128)(2,1)} all-gather(bf16[448,128]{1,0:T(8,128)(2,1)S(1)} %bitcast.10), channel_id=1, replica_groups=mesh['zh'=2,'y'=8,'x'=4,'zl'=4,'c'=2] {'x','c'}, dimensions={0}, use_global_device_ids=true | all-gather | bytes 1032192 | tf_op jit(solution)/shard_map/all_gather | solution.py:190
  39.7 28.7 %all-to-all-done.1 = bf16[8,8,64,256]{3,2,1,0:T(8,128)(2,1)S(1)} async-done(((bf16[8,8,64,256]{3,2,1,0:T(8,128)(2,1)}), bf16[8,8,64,256]{3,2,1,0:T(8,128)(2,1)S(1)}, u32[]{:S(2)}, u32[]{:S(2)}) %all-to-all-start.1) | async-done | bytes 2097184 | tf_op jit(solution)/shard_map/all_to_all | solution.py:184
  68.4 0.0 copy-start
  68.4 1.3 %copy-done = bf16[8,8,64,256]{3,2,1,0:T(8,128)(2,1)} copy-done((bf16[8,8,64,256]{3,2,1,0:T(8,128)(2,1)}, bf16[8,8,64,256]{3,2,1,0:T(8,128)(2,1)S(1)}, u32[]{:S(2)}) %copy-start) | copy-done | bytes 2097176
  69.7 20.9 %attend.1 = bf16[8,528,128]{2,1,0:T(8,128)(2,1)} custom-call(s32[5]{0:T(128)} %stack.23.at, bf16[3584,128]{1,0:T(8,128)(2,1)} %all_gather.3.q_ref, bf16[2,4,8,64,256]{4,3,2,1,0:T(8,128)(2,1)} %bitcast.8), custom_call_target="tpu_custom_call" | custom-call | tf_op jit(solution)/shard_map/attend/pallas_call | solution.py:196
  90.6 23.9 %all_to_all.16.got_ref = bf16[8,528,128]{2,1,0:T(8,128)(2,1)} all-to-all(bf16[8,528,128]{2,1,0:T(8,128)(2,1)} %attend.1), channel_id=1, replica_groups=mesh['zh'=2,'y'=8,'x'=4,'zl'=4,'c'=2] {'x','c'}, dimensions={0} | all-to-all | bytes 2162688 | tf_op jit(solution)/shard_map/all_to_all | solution.py:204
  114.5 3.2 %combine.1 = bf16[448,128]{1,0:T(8,128)(2,1)} custom-call(s32[5]{0:T(128)} %stack.23.at, bf16[448,128]{1,0:T(8,128)(2,1)} %bitcast.9, bf16[8,528,128]{2,1,0:T(8,128)(2,1)} %all_to_all.16.got_ref), custom_call_target="tpu_custom_call" | custom-call | tf_op jit(solution)/shard_map/combine/pallas_call | solution.py:205
  (1 shorter events, 0.0 us)
Async XLA Ops:
  17.1 6.5 %copy-start.1 = (bf16[7,64,128]{2,1,0:T(8,128)(2,1)S(1)}, bf16[7,64,128]{2,1,0:T(8,128)(2,1)}, u32[]{:S(2)}) copy-start(bf16[7,64,128]{2,1,0:T(8,128)(2,1)} %param.3) | copy-start | bytes 344068
  17.1 51.2 %all-to-all-start.1 = ((bf16[8,8,64,256]{3,2,1,0:T(8,128)(2,1)}), bf16[8,8,64,256]{3,2,1,0:T(8,128)(2,1)S(1)}, u32[]{:S(2)}, u32[]{:S(2)}) async-start(bf16[8,8,64,256]{3,2,1,0:T(8,128)(2,1)} %broadcast_in_dim.5), calls=%async_computation.1 | async-start | bytes 4194304 | tf_op jit(solution)/shard_map/all_to_all | solution.py:184
  68.4 1.3 %copy-start = (bf16[8,8,64,256]{3,2,1,0:T(8,128)(2,1)}, bf16[8,8,64,256]{3,2,1,0:T(8,128)(2,1)S(1)}, u32[]{:S(2)}) copy-start(bf16[8,8,64,256]{3,2,1,0:T(8,128)(2,1)S(1)} %all-to-all-done.1) | copy-start | bytes 6291460
